TPU v7x, 512 devices: a whole 4x8x8 slice. The times are simulated.
512 devices in a mesh: tile: 32 (over z, y_hi), col: 16 (over x, y_lo, core).
Axes of the slice: x: 4, y: 8 (y_hi: 4, y_lo: 2; y = y_hi * 2 + y_lo), z: 8, core: 2. Of those that a mesh axis runs over, the one named last changes fastest.
Arguments:
- latent: bfloat16 [32, 17, 4, 64, 256], P('tile', None, None, 'col'), may hold values from -20 to 20
- intersections: int32 [32], P('tile'), may hold values from 0 to 4, as said below
- norm_gain_one: float32 [256], replicated, may hold values from 0.5 to 1.5
- norm_shift_one: float32 [256], replicated, may hold values from -3 to 3
- weight_one: bfloat16 [3, 3, 3, 256, 256], P(None, None, None, 'col'), may hold values from -0.078125 to 0.078125
- norm_gain_two: float32 [256], replicated, may hold values from 0.5 to 1.5
- norm_shift_two: float32 [256], replicated, may hold values from -3 to 3
- weight_two: bfloat16 [3, 3, 3, 256, 256], P(None, None, None, 'col'), may hold values from -0.078125 to 0.078125
- conv_bias: float32 [256], replicated, may hold values from -1.8 to 1.8
Outputs:
- blended: bfloat16 [32, 17, 4, 64, 256], P('tile', None, None, 'col')
Inputs may be any that keep to these rules, and one draw needn't show every extreme that they name: intersections[0] is 0 and every other entry is 1 to 4; some entry equals 4.
All inputs are finite; a program needn't handle non-finite values.
Results may differ from a plain program's by a relative error of at most 0.0055.
Values may be sent and summed in bfloat16 or wider, within the bound.
No kernel may reach another device: no remote copies, remote signals or barrier semaphores. Data moves between devices by JAX's collectives and lax.ppermute only.
A program may use at most 64 MiB of HBM per device.

v0:
```python
import jax
import jax.numpy as jnp
from jax import lax
from jax.sharding import PartitionSpec as P

GROUPS = 32
OVMAX = 4
epsilon = 1e-06


def copy_for_each(array, axis):
    copies = jnp.broadcast_to(array, (lax.axis_size(axis), *array.shape))
    return lax.all_to_all(copies, axis, split_axis=0, concat_axis=0, tiled=True)


def over_copies(array, axis):
    return copy_for_each(array, axis).sum(axis=0)


def together(arrays, axis):
    flat, at, gathered = (jnp.concatenate([a.reshape(-1) for a in arrays]), 0, [])
    so_far = over_copies(flat, axis)
    for a in arrays:
        gathered.append(so_far[at : at + a.size].reshape(a.shape))
        at += a.size
    return tuple(gathered)


def extended_2(array, sides, width):
    for axis, dim in sides:
        size, length = (lax.axis_size(axis), array.shape[dim])
        up = [(i, (i + 1) % size) for i in range(size - 1)]
        down = [(j, i) for i, j in up]
        last = lax.slice_in_dim(array, length - width, length, axis=dim)
        first = lax.slice_in_dim(array, 0, width, axis=dim)
        before = lax.ppermute(last, axis, up)
        after = lax.ppermute(first, axis, down)
        array = jnp.concatenate([before, array, after], axis=dim)
    return array


def shifted(block, axis, distance):
    devices = range(lax.axis_size(axis))
    route = [(i - distance, i) for i in devices if i - distance in devices]
    return lax.ppermute(block, axis, route)


def conv_taps(padded, kernel):
    frames = padded.shape[0]
    height = padded.shape[1]
    out_width = padded.shape[2] - 2
    channels = padded.shape[3]
    outputs = kernel.shape[4]
    padded = jnp.pad(padded, ((2, 0), (1, 1), (0, 0), (0, 0)))
    running = jnp.zeros((frames * height * out_width, outputs), jnp.float32)
    for tap_t in range(3):
        for tap_h in range(3):
            for tap_w in range(3):
                window = padded[
                    tap_t : tap_t + frames, tap_h : tap_h + height, tap_w : tap_w + out_width
                ]
                running = running + jnp.dot(
                    window.reshape(-1, channels),
                    kernel[tap_t, tap_h, tap_w],
                    preferred_element_type=jnp.float32,
                )
    return running.reshape(frames, height, out_width, outputs)


def group_total(values, per_group):
    return jnp.sum(values, axis=(0, 1, 2)).reshape(GROUPS, per_group).sum(axis=1)


def norm_silu(values, inner, gain, shift):
    channels = values.shape[3]
    per_group = channels // GROUPS
    members = inner.shape[0] * inner.shape[1] * inner.shape[2] * lax.axis_size("col") * per_group
    chan_sums = group_total(inner, per_group)
    chan_squares = group_total(inner * inner, per_group)
    totals, squares = together((chan_sums, chan_squares), "col")
    group_mean = totals / members
    spread = jnp.maximum(squares / members - group_mean * group_mean, 0.0)
    inv_std = lax.rsqrt(spread + epsilon)
    normed = (values - jnp.repeat(group_mean, per_group)) * jnp.repeat(
        inv_std, per_group
    ) * gain + shift
    return jax.nn.silu(normed).astype(jnp.bfloat16)


def shards(
    latent,
    intersections,
    norm_gain_one,
    norm_shift_one,
    weight_one,
    norm_gain_two,
    norm_shift_two,
    weight_two,
    conv_bias,
):
    source = latent[0]
    latent_full = source.astype(jnp.float32)
    act_one = norm_silu(latent_full, latent_full, norm_gain_one, norm_shift_one)
    kernel_one, kernel_two = (
        lax.all_gather(weight_one, "col", axis=3, tiled=True),
        lax.all_gather(weight_two, "col", axis=3, tiled=True),
    )
    margin = extended_2(act_one, (("col", 2),), 2)
    hidden = conv_taps(margin, kernel=kernel_one).astype(jnp.bfloat16)
    hidden_full = hidden.astype(jnp.float32)
    act_two = norm_silu(hidden_full, hidden_full[:, :, 1:-1], norm_gain_two, norm_shift_two)
    own_width = source.shape[2]
    position = lax.axis_index("col") * own_width - 1 + jnp.arange(own_width + 2, dtype=jnp.int32)
    inside = (position >= 0) & (position < own_width * lax.axis_size("col"))
    act_two = jnp.where(inside[None, None, :, None], act_two, jnp.zeros_like(act_two))
    branch = conv_taps(act_two, kernel=kernel_two)
    decoded = (latent_full + (branch + conv_bias)).astype(jnp.bfloat16)
    frames = decoded.shape[0]
    received = shifted(decoded[frames - OVMAX :], "tile", 1)
    shared = intersections[0]
    extended = jnp.concatenate([received, jnp.zeros_like(received)], axis=0)
    aligned = lax.dynamic_slice_in_dim(extended, OVMAX - shared, OVMAX, 0)
    position_t = jnp.arange(OVMAX, dtype=jnp.int32)
    own_share = ((position_t + 1).astype(jnp.float32) / (shared + 1).astype(jnp.float32))[
        :, None, None, None
    ]
    head = decoded[:OVMAX].astype(jnp.float32)
    active = (position_t < shared)[:, None, None, None]
    mixed = jnp.where(
        active, own_share * head + (1.0 - own_share) * aligned.astype(jnp.float32), head
    )
    blended = jnp.concatenate([mixed.astype(jnp.bfloat16), decoded[OVMAX:]], axis=0)
    return blended[None]


def solution(mesh):
    in_specs = (
        P("tile", None, None, "col", None),
        P("tile"),
        P(),
        P(),
        P(None, None, None, "col", None),
        P(),
        P(),
        P(None, None, None, "col", None),
        P(),
    )
    out_specs = P("tile", None, None, "col", None)
    return jax.shard_map(shards, mesh=mesh, in_specs=in_specs, out_specs=out_specs, check_vma=False)
```

profile of v0, /device:TPU:64, one launch (start us, length us, event | category | flops | bytes accessed | tf_op | source)
XLA Modules:
  0.0 126.9 jit_solution(7533719370882032942)
XLA Ops:
  10.4 5.4 %all-to-all-start = ((f32[16,1,64]{2,1,0:T(1,128)}), f32[16,1,64]{2,1,0:T(1,128)S(1)}, u32[]{:S(2)}, u32[]{:S(2)}) async-start(f32[16,1,64]{2,1,0:T(1,128)} %broadcast_in_dim.51), calls=%async_computation | async-start | bytes 16384 | tf_op jit(solution)/shard_map/all_to_all | solution.py:13
  17.2 4.6 %all-to-all-done = f32[16,1,64]{2,1,0:T(1,128)S(1)} async-done(((f32[16,1,64]{2,1,0:T(1,128)}), f32[16,1,64]{2,1,0:T(1,128)S(1)}, u32[]{:S(2)}, u32[]{:S(2)}) %all-to-all-start) | async-done | bytes 4128 | tf_op jit(solution)/shard_map/all_to_all | solution.py:13
  23.5 1.8 %collective-permute-start = (bf16[17,4,2,256]{3,2,1,0:T(2,128)(2,1)S(1)}, bf16[17,4,2,256]{3,2,1,0:T(2,128)(2,1)S(1)}, u32[]{:S(2)}, u32[]{:S(2)}) collective-permute-start(bf16[17,4,2,256]{3,2,1,0:T(2,128)(2,1)S(1)} %get-tuple-element.61), channel_id=1, source_target_pairs={{0,1},{1,2},{2,3},{3,4},{4,5},{5,6},{6,7},{7,8},{8,9},{9,10},{10,1... | collective-permute-start | bytes 208904 | tf_op jit(solution)/shard_map/ppermute | solution.py:36
  27.1 1.7 %collective-permute-done.1 = bf16[17,4,2,256]{3,2,1,0:T(2,128)(2,1)S(1)} collective-permute-done((bf16[17,4,2,256]{3,2,1,0:T(2,128)(2,1)S(1)}, bf16[17,4,2,256]{3,2,1,0:T(2,128)(2,1)S(1)}, u32[]{:S(2)}, u32[]{:S(2)}) %collective-permute-start.1) | collective-permute-done | bytes 69664 | tf_op jit(solution)/shard_map/ppermute | solution.py:37
  29.4 2.0 %pad_slice_fusion.24 = (bf16[17,4,6,256]{3,2,1,0:T(8,128)(2,1)S(1)}, bf16[17,4,6,256]{3,2,1,0:T(8,128)(2,1)}, bf16[17,4,6,256]{3,2,1,0:T(8,128)(2,1)}, bf16[17,4...) fusion(bf16[17,4,8,256]{3,2,1,0:T(8,128)(2,1)S(1)} %pad_maximum, ...), kind=kLoop, calls=%fused_computation.24 | loop fusion | bytes 4247552 | tf_op jit(solution)/shard_map/slice | solution.py:59
  31.7 1.7 %reshape.223 = bf16[408,256]{1,0:T(8,128)(2,1)} reshape(bf16[17,4,6,256]{3,2,1,0:T(8,128)(2,1)} %get-tuple-element.35) | data formatting | bytes 417792 | tf_op jit(solution)/shard_map/reshape | solution.py:63
  34.2 1.7 %reshape.224 = bf16[408,256]{1,0:T(8,128)(2,1)} reshape(bf16[17,4,6,256]{3,2,1,0:T(8,128)(2,1)} %get-tuple-element.36) | data formatting | bytes 417792 | tf_op jit(solution)/shard_map/reshape | solution.py:63
  36.0 1.7 %reshape.225 = bf16[408,256]{1,0:T(8,128)(2,1)} reshape(bf16[17,4,6,256]{3,2,1,0:T(8,128)(2,1)} %get-tuple-element.37) | data formatting | bytes 417792 | tf_op jit(solution)/shard_map/reshape | solution.py:63
  37.7 1.7 %reshape.226 = bf16[408,256]{1,0:T(8,128)(2,1)} reshape(bf16[17,4,6,256]{3,2,1,0:T(8,128)(2,1)} %get-tuple-element.38) | data formatting | bytes 417792 | tf_op jit(solution)/shard_map/reshape | solution.py:63
  39.4 1.7 %reshape.227 = bf16[408,256]{1,0:T(8,128)(2,1)} reshape(bf16[17,4,6,256]{3,2,1,0:T(8,128)(2,1)} %get-tuple-element.39) | data formatting | bytes 417792 | tf_op jit(solution)/shard_map/reshape | solution.py:63
  41.1 1.7 %reshape.228 = bf16[408,256]{1,0:T(8,128)(2,1)} reshape(bf16[17,4,6,256]{3,2,1,0:T(8,128)(2,1)} %get-tuple-element.40) | data formatting | bytes 417792 | tf_op jit(solution)/shard_map/reshape | solution.py:63
  42.8 1.7 %reshape.229 = bf16[408,256]{1,0:T(8,128)(2,1)} reshape(bf16[17,4,6,256]{3,2,1,0:T(8,128)(2,1)} %get-tuple-element.41) | data formatting | bytes 417792 | tf_op jit(solution)/shard_map/reshape | solution.py:63
  44.6 1.7 %reshape.230 = bf16[408,256]{1,0:T(8,128)(2,1)} reshape(bf16[17,4,6,256]{3,2,1,0:T(8,128)(2,1)} %get-tuple-element.42) | data formatting | bytes 417792 | tf_op jit(solution)/shard_map/reshape | solution.py:63
  46.3 1.7 %reshape.231 = bf16[408,256]{1,0:T(8,128)(2,1)} reshape(bf16[17,4,6,256]{3,2,1,0:T(8,128)(2,1)} %get-tuple-element.43) | data formatting | bytes 417792 | tf_op jit(solution)/shard_map/reshape | solution.py:63
  48.0 1.7 %reshape.232 = bf16[408,256]{1,0:T(8,128)(2,1)} reshape(bf16[17,4,6,256]{3,2,1,0:T(8,128)(2,1)} %get-tuple-element.44) | data formatting | bytes 417792 | tf_op jit(solution)/shard_map/reshape | solution.py:63
  49.7 1.7 %reshape.233 = bf16[408,256]{1,0:T(8,128)(2,1)} reshape(bf16[17,4,6,256]{3,2,1,0:T(8,128)(2,1)} %get-tuple-element.45) | data formatting | bytes 417792 | tf_op jit(solution)/shard_map/reshape | solution.py:63
  51.5 1.7 %reshape.234 = bf16[408,256]{1,0:T(8,128)(2,1)} reshape(bf16[17,4,6,256]{3,2,1,0:T(8,128)(2,1)} %get-tuple-element.46) | data formatting | bytes 417792 | tf_op jit(solution)/shard_map/reshape | solution.py:63
  57.3 1.4 %fusion.17 = f32[408,256]{1,0:T(8,128)S(1)} fusion(bf16[408,256]{1,0:T(8,128)(2,1)} %reshape.223, bf16[3,3,3,256,256]{4,3,2,1,0:T(8,128)(2,1)} %all-gather.3.cloned.1.call-done), kind=kOutput, calls=%fused_computation.178 | convolution fusion | flops 53477376 | bytes 757760 | tf_op jit(solution)/shard_map/dot_general | solution.py:62
  70.3 8.9 %all-to-all-start.1 = ((f32[16,1,64]{2,1,0:T(1,128)}), f32[16,1,64]{2,1,0:T(1,128)S(1)}, u32[]{:S(2)}, u32[]{:S(2)}) async-start(f32[16,1,64]{2,1,0:T(1,128)} %broadcast_in_dim.54), calls=%async_computation.1 | async-start | bytes 16384 | tf_op jit(solution)/shard_map/all_to_all | solution.py:13
  79.2 6.0 %all-to-all-done.1 = f32[16,1,64]{2,1,0:T(1,128)S(1)} async-done(((f32[16,1,64]{2,1,0:T(1,128)}), f32[16,1,64]{2,1,0:T(1,128)S(1)}, u32[]{:S(2)}, u32[]{:S(2)}) %all-to-all-start.1) | async-done | bytes 4128 | tf_op jit(solution)/shard_map/all_to_all | solution.py:13
  93.7 5.8 %all-gather.5.cloned.1.call-done = bf16[3,3,3,256,256]{4,3,2,1,0:T(8,128)(2,1)} async-done(((bf16[3,3,3,16,256]{4,3,2,1,0:T(8,128)(2,1)}), bf16[3,3,3,256,256]{4,3,2,1,0:T(8,128)(2,1)}) %all-gather.5.cloned.1.call-update) | async-done | bytes 3538960 | tf_op jit(solution)/shard_map/all_gather | solution.py:106
  99.5 1.3 %fusion.14 = f32[272,256]{1,0:T(8,128)S(1)} fusion(bf16[272,256]{1,0:T(8,128)(2,1)} %reshape.251, bf16[3,3,3,256,256]{4,3,2,1,0:T(8,128)(2,1)} %all-gather.5.cloned.1.call-done), kind=kOutput, calls=%fused_computation.149 | convolution fusion | flops 35651584 | bytes 548864 | tf_op jit(solution)/shard_map/dot_general | solution.py:62
  110.0 4.3 %collective-permute-start.2 = (bf16[4,4,4,256]{3,2,1,0:T(4,128)(2,1)S(1)}, bf16[4,4,4,256]{3,2,1,0:T(4,128)(2,1)S(1)}, u32[]{:S(2)}, u32[]{:S(2)}) collective-permute-start(bf16[4,4,4,256]{3,2,1,0:T(4,128)(2,1)S(1)} %slice.536), channel_id=1, source_target_pairs={{0,16},{16,32},{32,48},{48,64},{64,80},{80,96},{96,112},{112,128},... | collective-permute-start | bytes 98312 | tf_op jit(solution)/shard_map/ppermute | solution.py:45
  114.4 4.8 %collective-permute-done.2 = bf16[4,4,4,256]{3,2,1,0:T(4,128)(2,1)S(1)} collective-permute-done((bf16[4,4,4,256]{3,2,1,0:T(4,128)(2,1)S(1)}, bf16[4,4,4,256]{3,2,1,0:T(4,128)(2,1)S(1)}, u32[]{:S(2)}, u32[]{:S(2)}) %collective-permute-start.2) | collective-permute-done | bytes 32800 | tf_op jit(solution)/shard_map/ppermute | solution.py:45
  (194 shorter events, 43.3 us)
Async XLA Ops:
  6.5 50.8 %all-gather.3.cloned.1.call-start = ((), (), s32[]{:S(2)}) async-start(), calls=%async_computation.2 | async-start | bytes 3760128 | tf_op jit(solution)/shard_map/all_gather | solution.py:105
  10.4 11.4 %all-to-all-start = ((f32[16,1,64]{2,1,0:T(1,128)}), f32[16,1,64]{2,1,0:T(1,128)S(1)}, u32[]{:S(2)}, u32[]{:S(2)}) async-start(f32[16,1,64]{2,1,0:T(1,128)} %broadcast_in_dim.51), calls=%async_computation | async-start | bytes 16384 | tf_op jit(solution)/shard_map/all_to_all | solution.py:13
  15.8 83.7 %all-gather.5.cloned.1.call-start = ((), (), s32[]{:S(2)}) async-start(), calls=%async_computation.3 | async-start | bytes 3760128 | tf_op jit(solution)/shard_map/all_gather | solution.py:106
  23.5 3.6 %collective-permute-start = (bf16[17,4,2,256]{3,2,1,0:T(2,128)(2,1)S(1)}, bf16[17,4,2,256]{3,2,1,0:T(2,128)(2,1)S(1)}, u32[]{:S(2)}, u32[]{:S(2)}) collective-permute-start(bf16[17,4,2,256]{3,2,1,0:T(2,128)(2,1)S(1)} %get-tuple-element.61), channel_id=1, source_target_pairs={{0,1},{1,2},{2,3},{3,4},{4,5},{5,6},{6,7},{7,8},{8,9},{9,10},{10,1... | collective-permute-start | bytes 208904 | tf_op jit(solution)/shard_map/ppermute | solution.py:36
  25.3 3.5 %collective-permute-start.1 = (bf16[17,4,2,256]{3,2,1,0:T(2,128)(2,1)S(1)}, bf16[17,4,2,256]{3,2,1,0:T(2,128)(2,1)S(1)}, u32[]{:S(2)}, u32[]{:S(2)}) collective-permute-start(bf16[17,4,2,256]{3,2,1,0:T(2,128)(2,1)S(1)} %get-tuple-element.62), channel_id=1, source_target_pairs={{1,0},{2,1},{3,2},{4,3},{5,4},{6,5},{7,6},{8,7},{9,8},{10,9},{11,1... | collective-permute-start | bytes 208904 | tf_op jit(solution)/shard_map/ppermute | solution.py:37
  34.2 18.9 %copy-start.3 = (bf16[17,4,6,256]{3,2,1,0:T(8,128)(2,1)S(1)}, bf16[17,4,6,256]{3,2,1,0:T(8,128)(2,1)}, u32[]{:S(2)}) copy-start(bf16[17,4,6,256]{3,2,1,0:T(8,128)(2,1)} %get-tuple-element.47) | copy-start | bytes 626692
  57.1 6.9 %copy-start.14 = (bf16[408,256]{1,0:T(8,128)(2,1)S(1)}, bf16[408,256]{1,0:T(8,128)(2,1)}, u32[]{:S(2)}) copy-start(bf16[408,256]{1,0:T(8,128)(2,1)} %reshape.226) | copy-start | bytes 626692
  57.3 6.9 %copy-start.13 = (bf16[408,256]{1,0:T(8,128)(2,1)S(1)}, bf16[408,256]{1,0:T(8,128)(2,1)}, u32[]{:S(2)}) copy-start(bf16[408,256]{1,0:T(8,128)(2,1)} %reshape.227) | copy-start | bytes 626692
  57.3 5.2 %copy-start.1 = (bf16[3,3,3,256,256]{4,3,2,1,0:T(8,128)(2,1)S(1)}, bf16[3,3,3,256,256]{4,3,2,1,0:T(8,128)(2,1)}, u32[]{:S(2)}) copy-start(bf16[3,3,3,256,256]{4,3,2,1,0:T(8,128)(2,1)} %all-gather.3.cloned.1.call-done) | copy-start | bytes 10616836
  57.3 6.4 %copy-start.15 = (bf16[408,256]{1,0:T(8,128)(2,1)S(1)}, bf16[408,256]{1,0:T(8,128)(2,1)}, u32[]{:S(2)}) copy-start(bf16[408,256]{1,0:T(8,128)(2,1)} %reshape.246) | copy-start | bytes 626692
  58.7 5.7 %copy-start.12 = (bf16[408,256]{1,0:T(8,128)(2,1)S(1)}, bf16[408,256]{1,0:T(8,128)(2,1)}, u32[]{:S(2)}) copy-start(bf16[408,256]{1,0:T(8,128)(2,1)} %reshape.228) | copy-start | bytes 626692
  61.2 3.5 %copy-start.11 = (bf16[408,256]{1,0:T(8,128)(2,1)S(1)}, bf16[408,256]{1,0:T(8,128)(2,1)}, u32[]{:S(2)}) copy-start(bf16[408,256]{1,0:T(8,128)(2,1)} %reshape.229) | copy-start | bytes 626692
  62.5 2.4 %copy-start.10 = (bf16[408,256]{1,0:T(8,128)(2,1)S(1)}, bf16[408,256]{1,0:T(8,128)(2,1)}, u32[]{:S(2)}) copy-start(bf16[408,256]{1,0:T(8,128)(2,1)} %reshape.230) | copy-start | bytes 626692
  64.0 1.5 %copy-start.8 = (bf16[408,256]{1,0:T(8,128)(2,1)S(1)}, bf16[408,256]{1,0:T(8,128)(2,1)}, u32[]{:S(2)}) copy-start(bf16[408,256]{1,0:T(8,128)(2,1)} %reshape.232) | copy-start | bytes 626692
  68.0 17.6 %copy-start.20 = (f32[256]{0:T(256)S(1)}, f32[256]{0:T(256)}, u32[]{:S(2)}) copy-start(f32[256]{0:T(256)} %param.15) | copy-start | bytes 3076
  68.0 17.6 %copy-start.21 = (f32[256]{0:T(256)S(1)}, f32[256]{0:T(256)}, u32[]{:S(2)}) copy-start(f32[256]{0:T(256)} %param.14) | copy-start | bytes 3076
  70.3 14.9 %all-to-all-start.1 = ((f32[16,1,64]{2,1,0:T(1,128)}), f32[16,1,64]{2,1,0:T(1,128)S(1)}, u32[]{:S(2)}, u32[]{:S(2)}) async-start(f32[16,1,64]{2,1,0:T(1,128)} %broadcast_in_dim.54), calls=%async_computation.1 | async-start | bytes 16384 | tf_op jit(solution)/shard_map/all_to_all | solution.py:13
  87.9 4.6 %copy-start.17 = (bf16[17,4,4,256]{3,2,1,0:T(4,128)(2,1)S(1)}, bf16[17,4,4,256]{3,2,1,0:T(4,128)(2,1)}, u32[]{:S(2)}) copy-start(bf16[17,4,4,256]{3,2,1,0:T(4,128)(2,1)} %get-tuple-element.32) | copy-start | bytes 417796
  87.9 4.7 %copy-start.16 = (bf16[17,4,4,256]{3,2,1,0:T(4,128)(2,1)S(1)}, bf16[17,4,4,256]{3,2,1,0:T(4,128)(2,1)}, u32[]{:S(2)}) copy-start(bf16[17,4,4,256]{3,2,1,0:T(4,128)(2,1)} %get-tuple-element.31) | copy-start | bytes 417796
  99.5 5.9 %copy-start = (bf16[3,3,3,256,256]{4,3,2,1,0:T(8,128)(2,1)S(1)}, bf16[3,3,3,256,256]{4,3,2,1,0:T(8,128)(2,1)}, u32[]{:S(2)}) copy-start(bf16[3,3,3,256,256]{4,3,2,1,0:T(8,128)(2,1)} %all-gather.5.cloned.1.call-done) | copy-start | bytes 10616836
  108.2 1.7 %copy-start.2 = (bf16[1,17,4,4,256]{4,3,2,1,0:T(4,128)(2,1)S(1)}, bf16[1,17,4,4,256]{4,3,2,1,0:T(4,128)(2,1)}, u32[]{:S(2)}) copy-start(bf16[1,17,4,4,256]{4,3,2,1,0:T(4,128)(2,1)} %param.9) | copy-start | bytes 417796
  108.2 1.7 %copy-start.22 = (f32[256]{0:T(256)S(1)}, f32[256]{0:T(256)}, u32[]{:S(2)}) copy-start(f32[256]{0:T(256)} %param.17) | copy-start | bytes 3076
  108.4 10.8 %copy-start.23 = (f32[4]{0:T(128)S(1)}, f32[4]{0:T(128)}, u32[]{:S(2)}) copy-start(f32[4]{0:T(128)} %get-tuple-element.68) | copy-start | bytes 52
  110.0 9.2 %collective-permute-start.2 = (bf16[4,4,4,256]{3,2,1,0:T(4,128)(2,1)S(1)}, bf16[4,4,4,256]{3,2,1,0:T(4,128)(2,1)S(1)}, u32[]{:S(2)}, u32[]{:S(2)}) collective-permute-start(bf16[4,4,4,256]{3,2,1,0:T(4,128)(2,1)S(1)} %slice.536), channel_id=1, source_target_pairs={{0,16},{16,32},{32,48},{48,64},{64,80},{80,96},{96,112},{112,128},... | collective-permute-start | bytes 98312 | tf_op jit(solution)/shard_map/ppermute | solution.py:45
  (7 other events, 9.1 us)
Sparse Core Ops, SparseCore 0:
  9.4 46.1 all-gather.2
  57.7 41.7 all-gather.4
where the time goes:
time: 128 us; the launch traced here: 127 us
  local copies, waits for them, and re-layouts  38.3 us (30%)
  waiting for transfers between devices  24.2 us (19%)
  starting transfers between devices  21.7 us (17%)
  matrix products  21.3 us (17%)
  between operations  15.1 us (12%)
  other arithmetic  6.35 us (5%)
    reshape x54, local copies, waits for them, and re-layouts, conv_taps(): window.reshape(-1, channels)  31 us
    dot_general x54, matrix products, conv_taps(): jnp.dot(window.reshape(-1, channels), kernel[tap_t, tap_h, tap_w], prefer...  21.3 us
    all_to_all x2, starting transfers between devices, copy_for_each(): return lax.all_to_all(copies, axis, split_axis=0, concat_axis=0, tiled=True)  14.3 us
    all_to_all x2, waiting for transfers between devices, copy_for_each(): return lax.all_to_all(copies, axis, split_axis=0, concat_axis=0, tiled=True)  10.6 us
    all_gather x1, waiting for transfers between devices, shards(): lax.all_gather(weight_two, 'col', axis=3, tiled=True)  5.76 us
    ppermute x1, waiting for transfers between devices, shifted(): return lax.ppermute(block, axis, route)  4.79 us
    slice x4, local copies, waits for them, and re-layouts, conv_taps(): padded[tap_t:tap_t + frames, tap_h:tap_h + height, tap_w:tap_w + out_width]  4.33 us
    ppermute x1, starting transfers between devices, shifted(): return lax.ppermute(block, axis, route)  4.3 us
  transfers between devices with their start and end apart: 7, of which 5 were waited for; matrix products, arithmetic and copies ran while one was open for 43% of the time, Pallas kernels for 0%

commit v1 on v0

--- a/solution.py
+++ b/solution.py
@@ -98,12 +98,22 @@
     weight_two,
     conv_bias,
 ):
+
+    def deliver_ranges(block_here, at_axis):
+        met_up = jnp.concatenate(
+            lax.all_to_all(
+                jnp.stack([block_here for _ in range(lax.axis_size("col"))]), "col", 0, 0
+            ),
+            at_axis,
+        )
+        return met_up
+
     source = latent[0]
     latent_full = source.astype(jnp.float32)
     act_one = norm_silu(latent_full, latent_full, norm_gain_one, norm_shift_one)
     kernel_one, kernel_two = (
         lax.all_gather(weight_one, "col", axis=3, tiled=True),
-        lax.all_gather(weight_two, "col", axis=3, tiled=True),
+        deliver_ranges(weight_two, 3),
     )
     margin = extended_2(act_one, (("col", 2),), 2)
     hidden = conv_taps(margin, kernel=kernel_one).astype(jnp.bfloat16)

time: 128 us -> 260 us (2.03)
  local copies, waits for them, and re-layouts: 38.3 us -> 115 us
  starting transfers between devices: 21.7 us -> 72.8 us
  other arithmetic: 6.35 us -> 15.2 us
  waiting for transfers between devices: 24.2 us -> 16.3 us
    reshape x54, local copies, waits for them, and re-layouts: 31 us -> 89.6 us  [conv_taps(): window.reshape(-1, channels)]
    all_to_all x2, starting transfers between devices: 14.3 us -> 61.7 us  [copy_for_each(): return lax.all_to_all(copies, axis, split_axis=0, concat_axis=0, tiled=True)]
    all_gather x1 -> x0, waiting for transfers between devices: 5.76 us -> none  [shards(): lax.all_gather(weight_two, 'col', axis=3, tiled=True)]
    slice x4, local copies, waits for them, and re-layouts: 4.33 us -> 8.85 us  [conv_taps(): padded[tap_t:tap_t + frames, tap_h:tap_h + height, tap_w:tap_w + out_width]]
    all_to_all x0 -> x1, starting transfers between devices: none -> 3.75 us  [deliver_ranges(): lax.all_to_all(jnp.stack([block_here for _ in range(lax.axis_size('col'))...]
    another operation x0 -> x1, local copies, waits for them, and re-layouts: none -> 2.9 us  [deliver_ranges(): jnp.stack([block_here for _ in range(lax.axis_size('col'))])]
    reduce_sum x7, other arithmetic: 2.66 us -> 5.41 us  [group_total(): jnp.sum(values, axis=(0, 1, 2)).reshape(GROUPS, per_group).sum(axis=1)]
  transfers between devices with their start and end apart: 7 -> 7, of which waited for: 5 -> 4; matrix products, arithmetic and copies ran while one was open for 43% -> 34% of each run, Pallas kernels for 0% -> 0%
where the time goes in v1:
time: 260 us; the launch traced here: 258 us
  local copies, waits for them, and re-layouts  115 us (44%)
  starting transfers between devices  72.8 us (28%)
  matrix products  22.7 us (9%)
  waiting for transfers between devices  16.3 us (6%)
  between operations  15.3 us (6%)
  other arithmetic  15.2 us (6%)
    reshape x54, local copies, waits for them, and re-layouts, conv_taps(): window.reshape(-1, channels)  89.6 us
    all_to_all x2, starting transfers between devices, copy_for_each(): return lax.all_to_all(copies, axis, split_axis=0, concat_axis=0, tiled=True)  61.7 us
    dot_general x54, matrix products, conv_taps(): jnp.dot(window.reshape(-1, channels), kernel[tap_t, tap_h, tap_w], prefer...  22.7 us
    slice x4, local copies, waits for them, and re-layouts, conv_taps(): padded[tap_t:tap_t + frames, tap_h:tap_h + height, tap_w:tap_w + out_width]  8.85 us
    all_to_all x2, waiting for transfers between devices, copy_for_each(): return lax.all_to_all(copies, axis, split_axis=0, concat_axis=0, tiled=True)  8.3 us
    reduce_sum x7, other arithmetic, group_total(): jnp.sum(values, axis=(0, 1, 2)).reshape(GROUPS, per_group).sum(axis=1)  5.41 us
  transfers between devices with their start and end apart: 7, of which 4 were waited for; matrix products, arithmetic and copies ran while one was open for 34% of the time, Pallas kernels for 0%

profile of v1, /device:TPU:64, one launch (start us, length us, event | category | flops | bytes accessed | tf_op | source)
XLA Modules:
  0.0 257.8 jit_solution(8607466924679936408)
XLA Ops:
  10.4 5.4 %all-to-all-start = ((f32[16,1,64]{2,1,0:T(1,128)}), f32[16,1,64]{2,1,0:T(1,128)S(1)}, u32[]{:S(2)}, u32[]{:S(2)}) async-start(f32[16,1,64]{2,1,0:T(1,128)} %broadcast_in_dim.51), calls=%async_computation | async-start | bytes 16384 | tf_op jit(solution)/shard_map/all_to_all | solution.py:13
  16.5 5.3 %all-to-all-done = f32[16,1,64]{2,1,0:T(1,128)S(1)} async-done(((f32[16,1,64]{2,1,0:T(1,128)}), f32[16,1,64]{2,1,0:T(1,128)S(1)}, u32[]{:S(2)}, u32[]{:S(2)}) %all-to-all-start) | async-done | bytes 4128 | tf_op jit(solution)/shard_map/all_to_all | solution.py:13
  21.8 2.9 %stack.2 = bf16[16,3,3,3,16,256]{5,4,3,2,1,0:T(8,128)(2,1)} broadcast(bf16[3,3,3,16,256]{4,3,2,1,0:T(8,128)(2,1)} %param.16), dimensions={1,2,3,4,5} | broadcast | bytes 3760128 | tf_op jit(solution)/shard_map/stack | solution.py:105
  24.7 3.8 %all-to-all-start.2 = ((bf16[16,3,3,3,16,256]{5,4,3,2,1,0:T(8,128)(2,1)}), bf16[16,3,3,3,16,256]{5,4,3,2,1,0:T(8,128)(2,1)S(1)}, u32[]{:S(2)}, u32[]{:S(2)}) async-start(bf16[16,3,3,3,16,256]{5,4,3,2,1,0:T(8,128)(2,1)} %stack.2), calls=%async_computation.2 | async-start | bytes 7077888 | tf_op jit(solution)/shard_map/all_to_all | solution.py:104
  32.4 2.2 collective-permute-start
  36.4 2.5 collective-permute-done.1
  40.4 2.5 pad_slice_fusion.24
  43.0 1.7 reshape.231
  44.7 2.9 %pad_slice_fusion.25 = (bf16[17,4,6,256]{3,2,1,0:T(8,128)(2,1)}, bf16[17,4,6,256]{3,2,1,0:T(8,128)(2,1)}, bf16[17,4,6,256]{3,2,1,0:T(8,128)(2,1)}, bf16[17,4,6,2...) fusion(bf16[17,4,8,256]{3,2,1,0:T(8,128)(2,1)} %copy-done.1), kind=kLoop, calls=%fused_computation.25 | loop fusion | bytes 1810432 | tf_op jit(solution)/shard_map/slice | solution.py:59
  47.6 1.7 reshape.230
  59.5 1.7 reshape.238
  74.9 1.7 reshape.247
  76.7 1.7 reshape.248
  78.4 1.7 reshape.249
  83.5 2.2 pad_maximum_fusion.2
  85.7 1.7 reshape.251
  107.0 1.9 reshape.289
  108.8 1.8 slice_reduce_fusion
  114.9 56.2 %all-to-all-start.1 = ((f32[16,1,64]{2,1,0:T(1,128)}), f32[16,1,64]{2,1,0:T(1,128)S(1)}, u32[]{:S(2)}, u32[]{:S(2)}) async-start(f32[16,1,64]{2,1,0:T(1,128)} %broadcast_in_dim.54), calls=%async_computation.1 | async-start | bytes 16384 | tf_op jit(solution)/shard_map/all_to_all | solution.py:13
  171.7 2.4 copy.14
  174.2 2.9 %all-to-all-done.1 = f32[16,1,64]{2,1,0:T(1,128)S(1)} async-done(((f32[16,1,64]{2,1,0:T(1,128)}), f32[16,1,64]{2,1,0:T(1,128)S(1)}, u32[]{:S(2)}, u32[]{:S(2)}) %all-to-all-start.1) | async-done | bytes 4128 | tf_op jit(solution)/shard_map/all_to_all | solution.py:13
  182.4 2.2 pad_slice_fusion
  241.2 3.9 %collective-permute-start.2 = (bf16[4,4,4,256]{3,2,1,0:T(4,128)(2,1)S(1)}, bf16[4,4,4,256]{3,2,1,0:T(4,128)(2,1)S(1)}, u32[]{:S(2)}, u32[]{:S(2)}) collective-permute-start(bf16[4,4,4,256]{3,2,1,0:T(4,128)(2,1)S(1)} %slice.536), channel_id=1, source_target_pairs={{0,16},{16,32},{32,48},{48,64},{64,80},{80,96},{96,112},{112,128},... | collective-permute-start | bytes 98312 | tf_op jit(solution)/shard_map/ppermute | solution.py:45
  245.2 4.8 %collective-permute-done.2 = bf16[4,4,4,256]{3,2,1,0:T(4,128)(2,1)S(1)} collective-permute-done((bf16[4,4,4,256]{3,2,1,0:T(4,128)(2,1)S(1)}, bf16[4,4,4,256]{3,2,1,0:T(4,128)(2,1)S(1)}, u32[]{:S(2)}, u32[]{:S(2)}) %collective-permute-start.2) | collective-permute-done | bytes 32800 | tf_op jit(solution)/shard_map/ppermute | solution.py:45
  (253 shorter events, 124.5 us)
Async XLA Ops:
  6.5 87.8 %all-gather.2.cloned.1.call-start = ((), (), s32[]{:S(2)}) async-start(), calls=%async_computation.3 | async-start | bytes 3760128 | tf_op jit(solution)/shard_map/all_gather | solution.py:115
  10.4 11.4 %all-to-all-start = ((f32[16,1,64]{2,1,0:T(1,128)}), f32[16,1,64]{2,1,0:T(1,128)S(1)}, u32[]{:S(2)}, u32[]{:S(2)}) async-start(f32[16,1,64]{2,1,0:T(1,128)} %broadcast_in_dim.51), calls=%async_computation | async-start | bytes 16384 | tf_op jit(solution)/shard_map/all_to_all | solution.py:13
  24.7 89.5 %all-to-all-start.2 = ((bf16[16,3,3,3,16,256]{5,4,3,2,1,0:T(8,128)(2,1)}), bf16[16,3,3,3,16,256]{5,4,3,2,1,0:T(8,128)(2,1)S(1)}, u32[]{:S(2)}, u32[]{:S(2)}) async-start(bf16[16,3,3,3,16,256]{5,4,3,2,1,0:T(8,128)(2,1)} %stack.2), calls=%async_computation.2 | async-start | bytes 7077888 | tf_op jit(solution)/shard_map/all_to_all | solution.py:104
  32.3 6.6 %copy-start.3 = (bf16[17,4,4,256]{3,2,1,0:T(4,128)(2,1)}, bf16[17,4,4,256]{3,2,1,0:T(4,128)(2,1)S(1)}, u32[]{:S(2)}) copy-start(bf16[17,4,4,256]{3,2,1,0:T(4,128)(2,1)S(1)} %fusion.12) | copy-start | bytes 417796
  32.4 4.0 %collective-permute-start = (bf16[17,4,2,256]{3,2,1,0:T(2,128)(2,1)S(1)}, bf16[17,4,2,256]{3,2,1,0:T(2,128)(2,1)S(1)}, u32[]{:S(2)}, u32[]{:S(2)}) collective-permute-start(bf16[17,4,2,256]{3,2,1,0:T(2,128)(2,1)S(1)} %get-tuple-element.61), channel_id=1, source_target_pairs={{0,1},{1,2},{2,3},{3,4},{4,5},{5,6},{6,7},{7,8},{8,9},{9,10},{10,1... | collective-permute-start | bytes 208904 | tf_op jit(solution)/shard_map/ppermute | solution.py:36
  34.6 4.3 %collective-permute-start.1 = (bf16[17,4,2,256]{3,2,1,0:T(2,128)(2,1)S(1)}, bf16[17,4,2,256]{3,2,1,0:T(2,128)(2,1)S(1)}, u32[]{:S(2)}, u32[]{:S(2)}) collective-permute-start(bf16[17,4,2,256]{3,2,1,0:T(2,128)(2,1)S(1)} %get-tuple-element.62), channel_id=1, source_target_pairs={{1,0},{2,1},{3,2},{4,3},{5,4},{6,5},{7,6},{8,7},{9,8},{10,9},{11,1... | collective-permute-start | bytes 208904 | tf_op jit(solution)/shard_map/ppermute | solution.py:37
  94.3 6.4 %copy-start.2 = (bf16[3,3,3,256,256]{4,3,2,1,0:T(8,128)(2,1)S(1)}, bf16[3,3,3,256,256]{4,3,2,1,0:T(8,128)(2,1)}, u32[]{:S(2)}) copy-start(bf16[3,3,3,256,256]{4,3,2,1,0:T(8,128)(2,1)} %all-gather.2.cloned.1.call-done) | copy-start | bytes 10616836
  94.3 6.5 %copy-start.25 = (bf16[408,256]{1,0:T(8,128)(2,1)S(1)}, bf16[408,256]{1,0:T(8,128)(2,1)}, u32[]{:S(2)}) copy-start(bf16[408,256]{1,0:T(8,128)(2,1)} %reshape.233) | copy-start | bytes 626692
  94.3 6.7 %copy-start.24 = (bf16[408,256]{1,0:T(8,128)(2,1)S(1)}, bf16[408,256]{1,0:T(8,128)(2,1)}, u32[]{:S(2)}) copy-start(bf16[408,256]{1,0:T(8,128)(2,1)} %reshape.234) | copy-start | bytes 626692
  94.3 6.9 %copy-start.23 = (bf16[408,256]{1,0:T(8,128)(2,1)S(1)}, bf16[408,256]{1,0:T(8,128)(2,1)}, u32[]{:S(2)}) copy-start(bf16[408,256]{1,0:T(8,128)(2,1)} %reshape.235) | copy-start | bytes 626692
  95.7 5.8 %copy-start.22 = (bf16[408,256]{1,0:T(8,128)(2,1)S(1)}, bf16[408,256]{1,0:T(8,128)(2,1)}, u32[]{:S(2)}) copy-start(bf16[408,256]{1,0:T(8,128)(2,1)} %reshape.236) | copy-start | bytes 626692
  114.2 56.9 %copy-start = (bf16[16,3,3,3,16,256]{5,4,3,2,1,0:T(8,128)(2,1)}, bf16[16,3,3,3,16,256]{5,4,3,2,1,0:T(8,128)(2,1)S(1)}, u32[]{:S(2)}) copy-start(bf16[16,3,3,3,16,256]{5,4,3,2,1,0:T(8,128)(2,1)S(1)} %all-to-all-done.2) | copy-start | bytes 10616836
  114.9 62.2 %all-to-all-start.1 = ((f32[16,1,64]{2,1,0:T(1,128)}), f32[16,1,64]{2,1,0:T(1,128)S(1)}, u32[]{:S(2)}, u32[]{:S(2)}) async-start(f32[16,1,64]{2,1,0:T(1,128)} %broadcast_in_dim.54), calls=%async_computation.1 | async-start | bytes 16384 | tf_op jit(solution)/shard_map/all_to_all | solution.py:13
  227.9 5.8 %copy-start.47 = (bf16[272,256]{1,0:T(8,128)(2,1)S(1)}, bf16[272,256]{1,0:T(8,128)(2,1)}, u32[]{:S(2)}) copy-start(bf16[272,256]{1,0:T(8,128)(2,1)} %reshape.266) | copy-start | bytes 417796
  227.9 6.0 %copy-start.46 = (bf16[272,256]{1,0:T(8,128)(2,1)S(1)}, bf16[272,256]{1,0:T(8,128)(2,1)}, u32[]{:S(2)}) copy-start(bf16[272,256]{1,0:T(8,128)(2,1)} %reshape.267) | copy-start | bytes 417796
  227.9 6.2 %copy-start.45 = (bf16[272,256]{1,0:T(8,128)(2,1)S(1)}, bf16[272,256]{1,0:T(8,128)(2,1)}, u32[]{:S(2)}) copy-start(bf16[272,256]{1,0:T(8,128)(2,1)} %reshape.268) | copy-start | bytes 417796
  227.9 6.4 %copy-start.44 = (bf16[272,256]{1,0:T(8,128)(2,1)S(1)}, bf16[272,256]{1,0:T(8,128)(2,1)}, u32[]{:S(2)}) copy-start(bf16[272,256]{1,0:T(8,128)(2,1)} %reshape.269) | copy-start | bytes 417796
  227.9 6.7 %copy-start.43 = (bf16[272,256]{1,0:T(8,128)(2,1)S(1)}, bf16[272,256]{1,0:T(8,128)(2,1)}, u32[]{:S(2)}) copy-start(bf16[272,256]{1,0:T(8,128)(2,1)} %reshape.270) | copy-start | bytes 417796
  229.1 5.7 %copy-start.42 = (bf16[272,256]{1,0:T(8,128)(2,1)S(1)}, bf16[272,256]{1,0:T(8,128)(2,1)}, u32[]{:S(2)}) copy-start(bf16[272,256]{1,0:T(8,128)(2,1)} %reshape.271) | copy-start | bytes 417796
  230.2 4.8 %copy-start.41 = (bf16[272,256]{1,0:T(8,128)(2,1)S(1)}, bf16[272,256]{1,0:T(8,128)(2,1)}, u32[]{:S(2)}) copy-start(bf16[272,256]{1,0:T(8,128)(2,1)} %reshape.272) | copy-start | bytes 417796
  231.4 3.8 %copy-start.40 = (bf16[272,256]{1,0:T(8,128)(2,1)S(1)}, bf16[272,256]{1,0:T(8,128)(2,1)}, u32[]{:S(2)}) copy-start(bf16[272,256]{1,0:T(8,128)(2,1)} %reshape.273) | copy-start | bytes 417796
  237.0 13.1 %copy-start.51 = (f32[4]{0:T(128)S(1)}, f32[4]{0:T(128)}, u32[]{:S(2)}) copy-start(f32[4]{0:T(128)} %get-tuple-element.67) | copy-start | bytes 52
  237.0 13.1 %copy-start.52 = (f32[4]{0:T(128)S(1)}, f32[4]{0:T(128)}, u32[]{:S(2)}) copy-start(f32[4]{0:T(128)} %get-tuple-element.68) | copy-start | bytes 52
  241.2 8.8 %collective-permute-start.2 = (bf16[4,4,4,256]{3,2,1,0:T(4,128)(2,1)S(1)}, bf16[4,4,4,256]{3,2,1,0:T(4,128)(2,1)S(1)}, u32[]{:S(2)}, u32[]{:S(2)}) collective-permute-start(bf16[4,4,4,256]{3,2,1,0:T(4,128)(2,1)S(1)} %slice.536), channel_id=1, source_target_pairs={{0,16},{16,32},{32,48},{48,64},{64,80},{80,96},{96,112},{112,128},... | collective-permute-start | bytes 98312 | tf_op jit(solution)/shard_map/ppermute | solution.py:45
  (36 other events, 64.8 us)
Sparse Core Ops, SparseCore 0:
  9.4 81.4 all-gather.1
